TPU v7x, 32 devices: a whole 2x2x4 slice. The times are simulated.
32 devices in a mesh: row: 4 (over z), col: 8 (over y, x, core).
Axes of the slice: x: 2, y: 2, z: 4, core: 2. Of those that a mesh axis runs over, the one named last changes fastest.
Arguments:
- features: bfloat16 [32768, 256], P(('row', 'col')), may hold values from -6 to 6
- tile_values: bfloat16 [4, 8, 256, 128, 128], P('row', 'col'), may hold values from -0.09375 to 0.09375
- tile_rows: int32 [4, 8, 256], P('row', 'col'), may hold values from 0 to 63, as said below
- tile_cols: int32 [4, 8, 256], P('row', 'col'), may hold values from 0 to 31, as said below
- tile_count: int32 [4, 8], P('row', 'col'), may hold values from 64 to 256, as said below
- w_first: bfloat16 [256, 256], replicated, may hold values from -0.375 to 0.375
- w_second: bfloat16 [256, 256], replicated, may hold values from -0.375 to 0.375
Outputs:
- output: bfloat16 [32768, 256], P(('row', 'col'))
Inputs may be any that keep to these rules, and one draw needn't show every extreme that they name: `tile_rows`: in each block the slots name distinct tiles; the first tile_count slots are ordered by tile column, then tile row; later slots are padding. `tile_cols`: as for tile_rows. `tile_count`: some block uses all 256 slots.
All inputs are finite; a program needn't handle non-finite values.
Results may differ from a plain program's by a relative error of at most 0.024.
Values may be sent and summed in bfloat16 or wider, within the bound.
A program may use at most 192 MiB of HBM per device.

v0:
```python
import functools

import jax
import jax.numpy as jnp
from jax import lax
from jax.experimental import pallas as pl
from jax.experimental.pallas import tpu as pltpu
from jax.sharding import PartitionSpec as P

LANES = 128
UNROLL = 8
LOADS = 4
PARTS = 2
ROWS_AT_ONCE = 256
MESH = pl.DeviceIdType.MESH


def iota(shape, axis):
    return lax.broadcasted_iota(jnp.int32, shape, axis)


def pair_plan(row_ids, col_ids, filled, row_tiles, pairs_total, width):
    slots = row_ids.shape[1]
    one, zero = jnp.int32(1), jnp.int32(0)

    def down(mask):
        return jnp.sum(mask, axis=0, keepdims=True)

    def across(mask):
        return jnp.sum(mask, axis=1, keepdims=True)

    square = (slots, slots)
    lane, sub = iota(square, 1), iota(square, 0)
    rows_l = jnp.where(iota((1, slots), 1) < filled, row_ids, -1)
    rows_s = across(jnp.where(lane == sub, rows_l, zero))
    cols_s = across(jnp.where(lane == sub, col_ids, zero))
    rank_s = across(jnp.where((rows_s == rows_l) & (lane < sub), one, zero))
    hit = jnp.where(rows_s == iota((slots, row_tiles), 1), one, zero)
    hit_t = jnp.where(rows_l == iota((row_tiles, slots), 0), one, zero)
    count_l, count_s = down(hit), across(hit_t)
    pairs_l, pairs_s = (count_l + 1) >> 1, (count_s + 1) >> 1
    box = (row_tiles, row_tiles)
    start_l = down(jnp.where(iota(box, 0) < iota(box, 1), pairs_s, zero))
    start_s = across(jnp.where(iota(box, 1) < iota(box, 0), pairs_l, zero))
    place_s = jnp.where(rows_s >= 0, 2 * across(hit * start_l) + rank_s, -one)
    here = place_s == iota((slots, width), 1)
    slot_ids = iota((slots, width), 0)
    slot_at = slots + down(jnp.where(here, slot_ids - slots, zero))
    col_at = down(jnp.where(here, cols_s, zero))
    opens = (start_s == iota((row_tiles, width), 1)) & (count_s > 0)
    keep = one - down(jnp.where(opens, one, zero))
    last = jnp.where(count_l > 0, start_l + pairs_l - 1, jnp.int32(pairs_total))
    return slot_at, col_at, keep.astype(jnp.float32), last


def kernel(n_row, n_col, chunks, pairs_total, filled, row_ids, col_ids, feat, w1, vals_hbm, out, *scratch):
    phases = 2 * chunks
    panels = scratch[:phases]
    core_in = scratch[phases : 2 * phases]
    step_in = scratch[2 * phases : 3 * phases]
    vals, sums, part, plan_v, keep_v, plan, keep, plan_sem = scratch[3 * phases : 3 * phases + 8]
    load_sem, g_send, g_recv, c_send, c_recv, s_send, s_recv = scratch[3 * phases + 8 :]
    slots, tile, _ = vals_hbm.shape
    node_dev, width = feat.shape
    per_dev = node_dev // tile
    half_tiles = per_dev // 2
    n_q = n_col // 2
    steps = n_q.bit_length() - 1
    block = half_tiles * tile
    half_rows = n_q * block
    r, c = lax.axis_index("row"), lax.axis_index("col")
    b0 = lax.rem(c, 2)
    q = lax.div(c, 2)

    barrier = pltpu.get_barrier_semaphore()
    partners = []
    for bit in range(steps + 1):
        mine = lax.rem(lax.div(c, 1 << bit), 2)
        partners.append((r, c + (1 - 2 * mine) * (1 << bit)))
    for device in partners:
        pl.semaphore_signal(barrier, inc=1, device_id=device, device_id_type=MESH)

    @pl.when(r > 0)
    def _():
        pl.semaphore_signal(barrier, inc=1, device_id=(r - 1, c), device_id_type=MESH)

    @pl.when(r < n_row - 1)
    def _():
        pl.semaphore_signal(barrier, inc=1, device_id=(r + 1, c), device_id_type=MESH)

    share = slots // LOADS
    loads = [
        pltpu.make_async_copy(
            vals_hbm.at[pl.ds(i * share, share)], vals.at[pl.ds(i * share, share)], load_sem.at[i]
        )
        for i in range(LOADS)
    ]
    for load in loads:
        load.start()

    def own(phase, offset, rows):
        return panels[phase].at[pl.ds(r * per_dev + offset, rows)]

    def project(chunk):
        def body(i, carry):
            at = pl.multiple_of(i * ROWS_AT_ONCE, ROWS_AT_ONCE)
            product = jnp.dot(
                feat[pl.ds(at, ROWS_AT_ONCE), :],
                w1[:, chunk * LANES : (chunk + 1) * LANES],
                preferred_element_type=jnp.float32,
            )
            tiles = ROWS_AT_ONCE // tile
            own(chunk, i * tiles, tiles)[...] = product.astype(jnp.bfloat16).reshape(
                tiles, tile, LANES
            )
            return carry

        lax.fori_loop(0, node_dev // ROWS_AT_ONCE, body, 0)

    project(0)
    neighbours = (r > 0).astype(jnp.int32) + (r < n_row - 1).astype(jnp.int32)
    pl.semaphore_wait(barrier, len(partners) + neighbours)

    cut = per_dev // PARTS

    def hop_copy(phase, way, hop, part_id, node, device):
        view = panels[phase].at[pl.ds(node * per_dev + part_id * cut, cut)]
        return pltpu.make_async_remote_copy(
            src_ref=view,
            dst_ref=view,
            send_sem=g_send.at[phase, way, hop - 1, part_id],
            recv_sem=g_recv.at[phase, way, hop - 1, part_id],
            device_id=(device, c),
            device_id_type=MESH,
        )

    def sends(phase, hop, k):
        yield (r < n_row - 1) & (r >= hop - 1), lambda: hop_copy(
            phase, 0, hop, k, r - hop + 1, r + 1
        )
        yield (r > 0) & (r + hop <= n_row), lambda: hop_copy(phase, 1, hop, k, r + hop - 1, r - 1)

    def hop_start(phase, hop, k):
        for cond, make in sends(phase, hop, k):

            @pl.when(cond)
            def _(make=make):
                make().start()

    def hop_wait(phase, hop, k):
        @pl.when(r >= hop)
        def _():
            hop_copy(phase, 0, hop, k, r - hop, r).wait_recv()

        @pl.when(r + hop < n_row)
        def _():
            hop_copy(phase, 1, hop, k, r + hop, r).wait_recv()

    def hop_drain(phase, hop, k):
        for cond, make in sends(phase, hop, k):

            @pl.when(cond)
            def _(make=make):
                make().wait_send()

    class Gather:
        def __init__(self, phase):
            self.phase, self.unit = phase, 0
            self.units = (n_row - 1) * PARTS if phase < phases else 0

        def advance(self, count=1):
            for _ in range(min(count, self.units - self.unit)):
                hop, k = self.unit // PARTS + 1, self.unit % PARTS
                if hop > 1:
                    hop_wait(self.phase, hop - 1, k)
                hop_start(self.phase, hop, k)
                self.unit += 1

        def send_all(self):
            self.advance(self.units)

        def finish(self):
            self.send_all()
            if self.units:
                for k in range(PARTS):
                    hop_wait(self.phase, n_row - 1, k)
                for hop in range(1, n_row):
                    for k in range(PARTS):
                        hop_drain(self.phase, hop, k)

    def compute(phase, low, high, total):
        panel = panels[phase]

        def one(p, acc):
            left = [vals[plan[0, 2 * p + k]] for k in range(2)]
            right = [panel[plan[1, 2 * p + k]] for k in range(2)]
            product = jnp.dot(
                jnp.concatenate(left, axis=1),
                jnp.concatenate(right, axis=0),
                preferred_element_type=jnp.float32,
            )
            acc = acc * keep[0, p] + product
            sums[p] = acc.astype(jnp.bfloat16)
            return acc

        def body(i, acc):
            for u in range(UNROLL):
                acc = one(i * UNROLL + u, acc)
            return acc

        return lax.fori_loop(low // UNROLL, high // UNROLL, body, total)

    def place_rows(parity):
        def body(i, carry):
            dq, h = lax.div(i, 2), lax.rem(i, 2)
            dest = 2 * dq + parity
            rev = sum(lax.rem(lax.div(dq, 1 << k), 2) * (1 << (steps - 1 - k)) for k in range(steps))
            at = rev * (1 - h) + dq * h
            base = ((parity * 2 + h) * n_q + at) * half_tiles
            for t in range(half_tiles):
                row_tile = dest * per_dev + h * half_tiles + t
                part[pl.ds(pl.multiple_of((base + t) * tile, tile), tile), :] = sums[
                    plan[2, row_tile]
                ]
            return carry

        lax.fori_loop(0, 2 * n_q, body, 0)

    def add_in(at, source, source_at, rows):
        piece = min(rows, ROWS_AT_ONCE)

        def body(i, carry):
            here = pl.ds(pl.multiple_of(at + i * piece, tile), piece)
            there = pl.ds(pl.multiple_of(source_at + i * piece, tile), piece)
            added = part[here, :].astype(jnp.float32) + source[there, :].astype(jnp.float32)
            part[here, :] = added.astype(jnp.bfloat16)
            return carry

        lax.fori_loop(0, rows // piece, body, 0)

    def remote(src, dst, send_sem, recv_sem, device):
        return pltpu.make_async_remote_copy(
            src_ref=src,
            dst_ref=dst,
            send_sem=send_sem,
            recv_sem=recv_sem,
            device_id=device,
            device_id_type=MESH,
        )

    def rows_at(ref, at, rows):
        return ref.at[pl.ds(pl.multiple_of(at, tile), rows)]

    def mine_at(h, step):
        return lax.rem(lax.div(q, 1 << (step if h == 0 else steps - 1 - step)), 2)

    def pieces(h, step, size):
        if step >= steps:
            return [(0, size)]
        mine = mine_at(h, step)
        return [((1 - mine) * (size // 2), size // 2), (mine * (size // 2), size // 2)]

    def reduce(phase, gather):
        place_rows(1 - b0)
        started = []
        cuts = [pieces(h, 0, half_rows) for h in range(2)]
        arrived = [[], []]
        for k in range(len(cuts[0])):
            for h in range(2):
                off, rows = cuts[h][k]
                copy = remote(
                    rows_at(part, ((1 - b0) * 2 + h) * half_rows + off, rows),
                    rows_at(core_in[phase], h * half_rows + off, rows),
                    c_send.at[phase, h, k],
                    c_recv.at[phase, h, k],
                    partners[0],
                )
                copy.start()
                started.append(copy)
                arrived[h].append((copy, core_in[phase], h * half_rows + off, off, rows))
        gather.advance()
        place_rows(b0)
        gather.advance()
        base = [(b0 * 2 + h) * half_rows for h in range(2)]

        def take(h, k):
            copy, source, source_at, off, rows = arrived[h][k]
            copy.wait_recv()
            add_in(base[h] + off, source, source_at, rows)

        size = half_rows
        for step in range(steps):
            following = [[], []]
            for h in range(2):
                take(h, 0)
                bit = step if h == 0 else steps - 1 - step
                away = base[h] + (1 - mine_at(h, step)) * (size // 2)
                landing = (h * (n_q - 1) + n_q - (n_q >> step)) * block
                for k, (off, rows) in enumerate(pieces(h, step + 1, size // 2)):
                    copy = remote(
                        rows_at(part, away + off, rows),
                        rows_at(step_in[phase], landing + off, rows),
                        s_send.at[phase, h, step, k],
                        s_recv.at[phase, h, step, k],
                        partners[1 + bit],
                    )
                    copy.start()
                    started.append(copy)
                    following[h].append((copy, step_in[phase], landing + off, off, rows))
            for h in range(2):
                take(h, 1)
                base[h] = base[h] + mine_at(h, step) * (size // 2)
            size //= 2
            arrived = following
            gather.advance()
        for h in range(2):
            copy, source, source_at, off, rows = arrived[h][0]
            copy.wait_recv()
            here = pl.ds(pl.multiple_of(base[h], tile), block)
            there = pl.ds(pl.multiple_of(source_at, tile), block)
            added = part[here, :].astype(jnp.float32) + source[there, :].astype(jnp.float32)
            if phase < chunks:
                hidden = jnp.maximum(added, 0.0).astype(jnp.bfloat16)
                own(phase + chunks, h * half_tiles, half_tiles)[...] = hidden.reshape(
                    half_tiles, tile, LANES
                )
            else:
                at = (phase - chunks) * LANES
                out[h * block : (h + 1) * block, at : at + LANES] = added.astype(jnp.bfloat16)
        return started

    vals[slots] = jnp.zeros((tile, tile), vals.dtype)
    sums[pairs_total] = jnp.zeros((tile, LANES), sums.dtype)
    gather = Gather(0)
    gather.advance(PARTS)
    for chunk in range(1, chunks):
        project(chunk)
    slot_at, col_at, keep_at, last = pair_plan(
        row_ids[...], col_ids[...], filled[0, 0], n_col * per_dev, pairs_total, plan.shape[1]
    )
    plan_v[0:1, :] = slot_at
    plan_v[1:2, :] = col_at
    plan_v[2:3, : last.shape[1]] = last
    keep_v[0:1, :] = keep_at
    moves = [
        pltpu.make_async_copy(plan_v, plan, plan_sem.at[0]),
        pltpu.make_async_copy(keep_v, keep, plan_sem.at[1]),
    ]
    gather.advance(PARTS)
    for move in moves:
        move.start()
    for move in moves:
        move.wait()
    for load in loads:
        load.wait()
    following = Gather(1)
    gather.send_all()
    following.advance(PARTS)
    gather.finish()
    for phase in range(phases):
        gather, following = following, Gather(phase + 2)
        middle = pairs_total // 2 // UNROLL * UNROLL
        total = compute(phase, 0, middle, jnp.zeros((tile, LANES), jnp.float32))
        gather.advance()
        compute(phase, middle, pairs_total, total)
        started = reduce(phase, gather)
        gather.send_all()
        following.advance(PARTS)
        for copy in started:
            copy.wait_send()
        gather.finish()


def shards(n_row, n_col, features, tile_values, tile_rows, tile_cols, tile_count, w_first, w_second):
    slots, tile = tile_values.shape[2], tile_values.shape[-1]
    node_dev, width = features.shape
    row_tiles = node_dev * n_col // tile
    chunks = width // LANES
    phases = 2 * chunks
    pairs_total = (slots + row_tiles) // 2
    n_q = n_col // 2
    steps = n_q.bit_length() - 1
    plan_width = -(-2 * pairs_total // LANES) * LANES
    half = node_dev // 2
    vmem = pl.BlockSpec(memory_space=pltpu.VMEM)
    smem = pl.BlockSpec(memory_space=pltpu.SMEM)
    bf16 = jnp.bfloat16
    dma = pltpu.SemaphoreType.DMA
    aggregate = pl.pallas_call(
        functools.partial(kernel, n_row, n_col, chunks, pairs_total),
        name="gcn",
        out_shape=jax.ShapeDtypeStruct((node_dev, width), bf16),
        in_specs=[smem] + [vmem] * 4 + [pl.BlockSpec(memory_space=pltpu.HBM)],
        out_specs=vmem,
        scratch_shapes=[pltpu.VMEM((n_row * node_dev // tile, tile, LANES), bf16)] * phases
        + [pltpu.VMEM((2 * n_q * half, LANES), bf16)] * phases
        + [pltpu.VMEM((2 * (n_q - 1) * half, LANES), bf16)] * phases
        + [
            pltpu.VMEM((slots + 1, tile, tile), bf16),
            pltpu.VMEM((pairs_total + 1, tile, LANES), bf16),
            pltpu.VMEM((n_col * node_dev, LANES), bf16),
            pltpu.VMEM((8, plan_width), jnp.int32),
            pltpu.VMEM((8, plan_width), jnp.float32),
            pltpu.SMEM((8, plan_width), jnp.int32),
            pltpu.SMEM((8, plan_width), jnp.float32),
            dma((2,)),
            dma((LOADS,)),
            dma((phases, 2, n_row - 1, PARTS)),
            dma((phases, 2, n_row - 1, PARTS)),
            dma((phases, 2, 2)),
            dma((phases, 2, 2)),
            dma((phases, 2, steps, 2)),
            dma((phases, 2, steps, 2)),
        ],
        compiler_params=pltpu.CompilerParams(
            collective_id=0, has_side_effects=True, vmem_limit_bytes=63 * 1024 * 1024
        ),
    )(tile_count, tile_rows[0], tile_cols[0], features, w_first, tile_values[0, 0])
    product = jnp.dot(aggregate, w_second, preferred_element_type=jnp.float32)
    return jax.nn.relu(product).astype(bf16)


def solution(mesh):
    return jax.shard_map(
        functools.partial(shards, mesh.shape["row"], mesh.shape["col"]),
        mesh=mesh,
        in_specs=(
            P(("row", "col"), None),
            P("row", "col", None, None, None),
            P("row", "col", None),
            P("row", "col", None),
            P("row", "col"),
            P(),
            P(),
        ),
        out_specs=P(("row", "col"), None),
        check_vma=False,
    )
```

profile of v0, /device:TPU:0, one launch (start us, length us, event | category | flops | bytes accessed | tf_op | source)
XLA Modules:
  0.0 107.3 jit_solution(15325543095110284703)
XLA Ops:
  0.0 0.0 copy-start
  0.7 104.5 %gcn.1 = bf16[1024,256]{1,0:T(8,128)(2,1)} custom-call(s32[1,1]{1,0:T(1,128)S(6)} %copy.8.filled, s32[1,256]{1,0:T(1,128)} %bitcast.6, s32[1,256]{1,0:T(1,128)} %bitcast.7, bf16[1024,256]{1,0:T(8,128)(2,1)} %feat.1, bf16[256,256]{1,0:T(8,128)(2,1)} %w1.1, bf16[256,128,128]{2,1,0:T(8,128)(2,1)} %bitcast.5), custom_call_target="tpu_custom_call" | custom-call | tf_op jit(solution)/shard_map/gcn/pallas_call | solution.py:389
  105.2 0.0 copy-done
  105.2 2.1 %fusion = bf16[1024,256]{1,0:T(8,128)(2,1)} fusion(bf16[1024,256]{1,0:T(8,128)(2,1)} %gcn.1, bf16[256,256]{1,0:T(8,128)(2,1)S(1)} %copy-done), kind=kOutput, calls=%fused_computation.1 | convolution fusion | flops 134742016 | bytes 1179648 | tf_op jit(solution)/shard_map/dot_general | solution.py:419
Async XLA Ops:
  0.0 105.2 %copy-start = (bf16[256,256]{1,0:T(8,128)(2,1)S(1)}, bf16[256,256]{1,0:T(8,128)(2,1)}, u32[]{:S(2)}) copy-start(bf16[256,256]{1,0:T(8,128)(2,1)} %param.13) | copy-start | bytes 393220
where the time goes:
time: 108 us; the launch traced here: 107 us
  Pallas kernels  105 us (97%)
  matrix products  2.13 us (2%)
    pallas_call x1, Pallas kernels, shards(): pl.pallas_call(functools.partial(kernel, n_row, n_col, chunks, pairs_tota...  105 us

commit v1 on v0

--- a/solution.py
+++ b/solution.py
@@ -8,7 +8,7 @@
 from jax.sharding import PartitionSpec as P
 
 LANES = 128
-UNROLL = 8
+UNROLL_PARTS = 2
 LOADS = 4
 PARTS = 2
 ROWS_AT_ONCE = 256
@@ -188,6 +188,8 @@
                     for k in range(PARTS):
                         hop_drain(self.phase, hop, k)
 
+    unroll = pairs_total // UNROLL_PARTS
+
     def compute(phase, low, high, total):
         panel = panels[phase]
 
@@ -204,11 +206,11 @@
             return acc
 
         def body(i, acc):
-            for u in range(UNROLL):
-                acc = one(i * UNROLL + u, acc)
+            for u in range(unroll):
+                acc = one(i * unroll + u, acc)
             return acc
 
-        return lax.fori_loop(low // UNROLL, high // UNROLL, body, total)
+        return lax.fori_loop(low // unroll, high // unroll, body, total)
 
     def place_rows(parity):
         def body(i, carry):
@@ -359,10 +361,10 @@
     gather.finish()
     for phase in range(phases):
         gather, following = following, Gather(phase + 2)
-        middle = pairs_total // 2 // UNROLL * UNROLL
+        middle = UNROLL_PARTS // 2 * unroll
         total = compute(phase, 0, middle, jnp.zeros((tile, LANES), jnp.float32))
         gather.advance()
-        compute(phase, middle, pairs_total, total)
+        compute(phase, middle, UNROLL_PARTS * unroll, total)
         started = reduce(phase, gather)
         gather.send_all()
         following.advance(PARTS)
@@ -377,7 +379,7 @@
     row_tiles = node_dev * n_col // tile
     chunks = width // LANES
     phases = 2 * chunks
-    pairs_total = (slots + row_tiles) // 2
+    pairs_total = -(-(slots + row_tiles) // (2 * UNROLL_PARTS)) * UNROLL_PARTS
     n_q = n_col // 2
     steps = n_q.bit_length() - 1
     plan_width = -(-2 * pairs_total // LANES) * LANES

time: 108 us -> 101 us (0.935)
  Pallas kernels: 105 us -> 98.1 us
    pallas_call x1, Pallas kernels: 105 us -> 98.1 us  [shards(): pl.pallas_call(functools.partial(kernel, n_row, n_col, chunks, pairs_tota...]
where the time goes in v1:
time: 101 us
  Pallas kernels  98.1 us (97%)
  matrix products  2.13 us (2%)
    pallas_call x1, Pallas kernels, shards(): pl.pallas_call(functools.partial(kernel, n_row, n_col, chunks, pairs_tota...  98.1 us
    dot_general x1, matrix products, shards(): product = jnp.dot(aggregate, w_second, preferred_element_type=jnp.float32)  2.13 us

profile of v1, /device:TPU:0, one launch (start us, length us, event | category | flops | bytes accessed | tf_op | source)
XLA Modules:
  0.0 101.0 jit_solution(625585726157883807)
XLA Ops:
  0.0 0.0 copy-start
  0.7 98.1 %gcn.1 = bf16[1024,256]{1,0:T(8,128)(2,1)} custom-call(s32[1,1]{1,0:T(1,128)S(6)} %copy.8.filled, s32[1,256]{1,0:T(1,128)} %bitcast.6, s32[1,256]{1,0:T(1,128)} %bitcast.7, bf16[1024,256]{1,0:T(8,128)(2,1)} %feat.1, bf16[256,256]{1,0:T(8,128)(2,1)} %w1.1, bf16[256,128,128]{2,1,0:T(8,128)(2,1)} %bitcast.5), custom_call_target="tpu_custom_call" | custom-call | tf_op jit(solution)/shard_map/gcn/pallas_call | solution.py:391
  98.8 0.0 copy-done
  98.8 2.1 %fusion = bf16[1024,256]{1,0:T(8,128)(2,1)} fusion(bf16[1024,256]{1,0:T(8,128)(2,1)} %gcn.1, bf16[256,256]{1,0:T(8,128)(2,1)S(1)} %copy-done), kind=kOutput, calls=%fused_computation.1 | convolution fusion | flops 134742016 | bytes 1179648 | tf_op jit(solution)/shard_map/dot_general | solution.py:421
Async XLA Ops:
  0.0 98.8 %copy-start = (bf16[256,256]{1,0:T(8,128)(2,1)S(1)}, bf16[256,256]{1,0:T(8,128)(2,1)}, u32[]{:S(2)}) copy-start(bf16[256,256]{1,0:T(8,128)(2,1)} %param.13) | copy-start | bytes 393220

commit v2 on v1

--- a/solution.py
+++ b/solution.py
@@ -53,13 +53,13 @@
     return slot_at, col_at, keep.astype(jnp.float32), last
 
 
-def kernel(n_row, n_col, chunks, pairs_total, filled, row_ids, col_ids, feat, w1, vals_hbm, out, *scratch):
+def kernel(n_row, n_col, chunks, pairs_total, filled, row_ids, col_ids, feat_hbm, w1_hbm, vals_hbm, out, *scratch):
     phases = 2 * chunks
     panels = scratch[:phases]
     core_in = scratch[phases : 2 * phases]
     step_in = scratch[2 * phases : 3 * phases]
-    vals, sums, part, plan_v, keep_v, plan, keep, plan_sem = scratch[3 * phases : 3 * phases + 8]
-    load_sem, g_send, g_recv, c_send, c_recv, s_send, s_recv = scratch[3 * phases + 8 :]
+    feat, w1, vals, sums, part, plan_v, keep_v, plan, keep, plan_sem = scratch[3 * phases : 3 * phases + 10]
+    in_sem, load_sem, g_send, g_recv, c_send, c_recv, s_send, s_recv = scratch[3 * phases + 10 :]
     slots, tile, _ = vals_hbm.shape
     node_dev, width = feat.shape
     per_dev = node_dev // tile
@@ -72,6 +72,19 @@
     b0 = lax.rem(c, 2)
     q = lax.div(c, 2)
 
+    cut = per_dev // PARTS
+    cut_rows = cut * tile
+    feat_loads = [
+        pltpu.make_async_copy(
+            feat_hbm.at[pl.ds(k * cut_rows, cut_rows)], feat.at[pl.ds(k * cut_rows, cut_rows)], in_sem.at[k + 1]
+        )
+        for k in range(PARTS)
+    ]
+    w1_load = pltpu.make_async_copy(w1_hbm, w1, in_sem.at[0])
+    w1_load.start()
+    for load in feat_loads:
+        load.start()
+
     barrier = pltpu.get_barrier_semaphore()
     partners = []
     for bit in range(steps + 1):
@@ -79,14 +92,25 @@
         partners.append((r, c + (1 - 2 * mine) * (1 << bit)))
     for device in partners:
         pl.semaphore_signal(barrier, inc=1, device_id=device, device_id_type=MESH)
-
-    @pl.when(r > 0)
-    def _():
-        pl.semaphore_signal(barrier, inc=1, device_id=(r - 1, c), device_id_type=MESH)
-
-    @pl.when(r < n_row - 1)
-    def _():
-        pl.semaphore_signal(barrier, inc=1, device_id=(r + 1, c), device_id_type=MESH)
+    greeted = jnp.int32(len(partners))
+    last_row = n_row - 1
+    distances = [d * sign for d in range(last_row, 0, -1) for sign in (1, -1)]
+
+    def inner(node):
+        return (node > 0) & (node < last_row)
+
+    def outer(node):
+        return (node == 0) | (node == last_row)
+
+    for d in distances:
+        there = r + d
+        valid = (there >= 0) & (there <= last_row)
+        reached = valid if abs(d) == 1 else valid & inner(there)
+        greeted = greeted + reached.astype(jnp.int32)
+
+        @pl.when(valid if abs(d) == 1 else valid & inner(r))
+        def _(there=there):
+            pl.semaphore_signal(barrier, inc=1, device_id=(there, c), device_id_type=MESH)
 
     share = slots // LOADS
     loads = [
@@ -101,96 +125,99 @@
     def own(phase, offset, rows):
         return panels[phase].at[pl.ds(r * per_dev + offset, rows)]
 
-    def project(chunk):
-        def body(i, carry):
-            at = pl.multiple_of(i * ROWS_AT_ONCE, ROWS_AT_ONCE)
+    def project(chunk, k):
+        size = min(cut_rows, ROWS_AT_ONCE)
+        for at in range(k * cut_rows, (k + 1) * cut_rows, size):
             product = jnp.dot(
-                feat[pl.ds(at, ROWS_AT_ONCE), :],
+                feat[at : at + size, :],
                 w1[:, chunk * LANES : (chunk + 1) * LANES],
                 preferred_element_type=jnp.float32,
             )
-            tiles = ROWS_AT_ONCE // tile
-            own(chunk, i * tiles, tiles)[...] = product.astype(jnp.bfloat16).reshape(
-                tiles, tile, LANES
-            )
-            return carry
-
-        lax.fori_loop(0, node_dev // ROWS_AT_ONCE, body, 0)
-
-    project(0)
-    neighbours = (r > 0).astype(jnp.int32) + (r < n_row - 1).astype(jnp.int32)
-    pl.semaphore_wait(barrier, len(partners) + neighbours)
-
-    cut = per_dev // PARTS
-
-    def hop_copy(phase, way, hop, part_id, node, device):
-        view = panels[phase].at[pl.ds(node * per_dev + part_id * cut, cut)]
+            tiles = size // tile
+            own(chunk, at // tile, tiles)[...] = product.astype(jnp.bfloat16).reshape(tiles, tile, LANES)
+
+    def node_copy(phase, origin, d, k, device):
+        view = panels[phase].at[pl.ds(origin * per_dev + k * cut, cut)]
         return pltpu.make_async_remote_copy(
             src_ref=view,
             dst_ref=view,
-            send_sem=g_send.at[phase, way, hop - 1, part_id],
-            recv_sem=g_recv.at[phase, way, hop - 1, part_id],
+            send_sem=g_send.at[phase, d + n_row - 1, k],
+            recv_sem=g_recv.at[phase, d + n_row - 1, k],
             device_id=(device, c),
             device_id_type=MESH,
         )
 
-    def sends(phase, hop, k):
-        yield (r < n_row - 1) & (r >= hop - 1), lambda: hop_copy(
-            phase, 0, hop, k, r - hop + 1, r + 1
-        )
-        yield (r > 0) & (r + hop <= n_row), lambda: hop_copy(phase, 1, hop, k, r + hop - 1, r - 1)
-
-    def hop_start(phase, hop, k):
-        for cond, make in sends(phase, hop, k):
-
-            @pl.when(cond)
-            def _(make=make):
-                make().start()
-
-    def hop_wait(phase, hop, k):
-        @pl.when(r >= hop)
-        def _():
-            hop_copy(phase, 0, hop, k, r - hop, r).wait_recv()
-
-        @pl.when(r + hop < n_row)
-        def _():
-            hop_copy(phase, 1, hop, k, r + hop, r).wait_recv()
-
-    def hop_drain(phase, hop, k):
-        for cond, make in sends(phase, hop, k):
-
-            @pl.when(cond)
-            def _(make=make):
-                make().wait_send()
-
-    class Gather:
-        def __init__(self, phase):
-            self.phase, self.unit = phase, 0
-            self.units = (n_row - 1) * PARTS if phase < phases else 0
-
-        def advance(self, count=1):
-            for _ in range(min(count, self.units - self.unit)):
-                hop, k = self.unit // PARTS + 1, self.unit % PARTS
-                if hop > 1:
-                    hop_wait(self.phase, hop - 1, k)
-                hop_start(self.phase, hop, k)
-                self.unit += 1
-
-        def send_all(self):
-            self.advance(self.units)
-
-        def finish(self):
-            self.send_all()
-            if self.units:
-                for k in range(PARTS):
-                    hop_wait(self.phase, n_row - 1, k)
-                for hop in range(1, n_row):
-                    for k in range(PARTS):
-                        hop_drain(self.phase, hop, k)
+    def inner_sends(phase, k):
+        for d in distances:
+            target = r + d
+            yield inner(target), node_copy(phase, r, d, k, target)
+
+    def outer_sends(phase, k):
+        for d in (1, -1):
+            target = r + d
+            yield outer(target), node_copy(phase, r, d, k, target)
+
+    def relays(phase, near, k):
+        for sign in (1, -1):
+            origin = r - sign * near
+            place = n_row - 2 if sign > 0 else 1
+            valid = (r == place) & (origin >= 0) & (origin <= last_row)
+            arrived = node_copy(phase, origin, sign * near, k, r)
+            forward = node_copy(phase, origin, sign * (near + 1), k, r + sign)
+            yield valid, arrived, forward
+
+    def start_all(sends):
+        for valid, copy in sends:
+            pl.when(valid)(copy.start)
+
+    def own_inner(phase):
+        if phase < phases:
+            for k in range(PARTS):
+                start_all(inner_sends(phase, k))
+
+    def own_outer(phase):
+        if phase < phases:
+            for k in range(PARTS):
+                start_all(outer_sends(phase, k))
+
+    def relay(phase, near, k):
+        if phase < phases:
+            for valid, arrived, forward in relays(phase, near, k):
+
+                @pl.when(valid)
+                def _(arrived=arrived, forward=forward):
+                    arrived.wait_recv()
+                    forward.start()
+
+    def relay_far(phase):
+        for k in range(PARTS):
+            for near in range(2, last_row):
+                relay(phase, near, k)
+
+    def relay_all(phase):
+        for k in range(PARTS):
+            for near in range(1, last_row):
+                relay(phase, near, k)
+
+    def gathered(phase):
+        for k in range(PARTS):
+            for d in sorted(distances, key=abs):
+                origin = r - d
+                relayed = r == (n_row - 2 if d > 0 else 1)
+                valid = (origin >= 0) & (origin <= last_row) & jnp.logical_not(relayed)
+                pl.when(valid)(node_copy(phase, origin, d, k, r).wait_recv)
+
+    def drain(phase):
+        for k in range(PARTS):
+            for valid, copy in [*inner_sends(phase, k), *outer_sends(phase, k)]:
+                pl.when(valid)(copy.wait_send)
+            for near in range(1, last_row):
+                for valid, _, forward in relays(phase, near, k):
+                    pl.when(valid)(forward.wait_send)
 
     unroll = pairs_total // UNROLL_PARTS
 
-    def compute(phase, low, high, total):
+    def compute(phase):
         panel = panels[phase]
 
         def one(p, acc):
@@ -210,15 +237,13 @@
                 acc = one(i * unroll + u, acc)
             return acc
 
-        return lax.fori_loop(low // unroll, high // unroll, body, total)
-
-    def place_rows(parity):
+        lax.fori_loop(0, UNROLL_PARTS, body, jnp.zeros((tile, LANES), jnp.float32))
+
+    def place_rows(parity, h, at, count):
         def body(i, carry):
-            dq, h = lax.div(i, 2), lax.rem(i, 2)
-            dest = 2 * dq + parity
-            rev = sum(lax.rem(lax.div(dq, 1 << k), 2) * (1 << (steps - 1 - k)) for k in range(steps))
-            at = rev * (1 - h) + dq * h
-            base = ((parity * 2 + h) * n_q + at) * half_tiles
+            rev = sum(lax.rem(lax.div(at + i, 1 << k), 2) * (1 << (steps - 1 - k)) for k in range(steps))
+            dest = 2 * (rev if h == 0 else at + i) + parity
+            base = ((parity * 2 + h) * n_q + at + i) * half_tiles
             for t in range(half_tiles):
                 row_tile = dest * per_dev + h * half_tiles + t
                 part[pl.ds(pl.multiple_of((base + t) * tile, tile), tile), :] = sums[
@@ -226,7 +251,7 @@
                 ]
             return carry
 
-        lax.fori_loop(0, 2 * n_q, body, 0)
+        lax.fori_loop(0, count, body, 0)
 
     def add_in(at, source, source_at, rows):
         piece = min(rows, ROWS_AT_ONCE)
@@ -262,14 +287,14 @@
         mine = mine_at(h, step)
         return [((1 - mine) * (size // 2), size // 2), (mine * (size // 2), size // 2)]
 
-    def reduce(phase, gather):
-        place_rows(1 - b0)
+    def reduce(phase):
         started = []
         cuts = [pieces(h, 0, half_rows) for h in range(2)]
         arrived = [[], []]
         for k in range(len(cuts[0])):
             for h in range(2):
                 off, rows = cuts[h][k]
+                place_rows(1 - b0, h, lax.div(off, block), rows // block)
                 copy = remote(
                     rows_at(part, ((1 - b0) * 2 + h) * half_rows + off, rows),
                     rows_at(core_in[phase], h * half_rows + off, rows),
@@ -280,9 +305,10 @@
                 copy.start()
                 started.append(copy)
                 arrived[h].append((copy, core_in[phase], h * half_rows + off, off, rows))
-        gather.advance()
-        place_rows(b0)
-        gather.advance()
+        for k in range(len(cuts[0])):
+            for h in range(2):
+                off, rows = cuts[h][k]
+                place_rows(b0, h, lax.div(off, block), rows // block)
         base = [(b0 * 2 + h) * half_rows for h in range(2)]
 
         def take(h, k):
@@ -314,7 +340,9 @@
                 base[h] = base[h] + mine_at(h, step) * (size // 2)
             size //= 2
             arrived = following
-            gather.advance()
+            if step == 0:
+                for k in range(PARTS):
+                    relay(phase + 1, 1, k)
         for h in range(2):
             copy, source, source_at, off, rows = arrived[h][0]
             copy.wait_recv()
@@ -331,12 +359,20 @@
                 out[h * block : (h + 1) * block, at : at + LANES] = added.astype(jnp.bfloat16)
         return started
 
+    w1_load.wait()
+    for k in range(PARTS):
+        feat_loads[k].wait()
+        project(0, k)
+        if k == 0:
+            pl.semaphore_wait(barrier, greeted)
+        start_all(inner_sends(0, k))
+        start_all(outer_sends(0, k))
+    for chunk in range(1, chunks):
+        for k in range(PARTS):
+            project(chunk, k)
+    pl.when(outer(r))(lambda: own_inner(1))
     vals[slots] = jnp.zeros((tile, tile), vals.dtype)
     sums[pairs_total] = jnp.zeros((tile, LANES), sums.dtype)
-    gather = Gather(0)
-    gather.advance(PARTS)
-    for chunk in range(1, chunks):
-        project(chunk)
     slot_at, col_at, keep_at, last = pair_plan(
         row_ids[...], col_ids[...], filled[0, 0], n_col * per_dev, pairs_total, plan.shape[1]
     )
@@ -348,29 +384,29 @@
         pltpu.make_async_copy(plan_v, plan, plan_sem.at[0]),
         pltpu.make_async_copy(keep_v, keep, plan_sem.at[1]),
     ]
-    gather.advance(PARTS)
     for move in moves:
         move.start()
+    relay_all(0)
     for move in moves:
         move.wait()
     for load in loads:
         load.wait()
-    following = Gather(1)
-    gather.send_all()
-    following.advance(PARTS)
-    gather.finish()
+    pl.when(inner(r))(lambda: own_inner(1))
+    own_outer(1)
     for phase in range(phases):
-        gather, following = following, Gather(phase + 2)
-        middle = UNROLL_PARTS // 2 * unroll
-        total = compute(phase, 0, middle, jnp.zeros((tile, LANES), jnp.float32))
-        gather.advance()
-        compute(phase, middle, UNROLL_PARTS * unroll, total)
-        started = reduce(phase, gather)
-        gather.send_all()
-        following.advance(PARTS)
+        gathered(phase)
+        compute(phase)
+        started = reduce(phase)
+        if phase < chunks:
+            own_inner(phase + chunks)
+        if phase + 1 < phases:
+            relay_far(phase + 1)
+        if phase < chunks:
+            own_outer(phase + chunks)
         for copy in started:
             copy.wait_send()
-        gather.finish()
+    for phase in range(phases):
+        drain(phase)
 
 
 def shards(n_row, n_col, features, tile_values, tile_rows, tile_cols, tile_count, w_first, w_second):
@@ -391,13 +427,15 @@
     aggregate = pl.pallas_call(
         functools.partial(kernel, n_row, n_col, chunks, pairs_total),
         name="gcn",
-        out_shape=jax.ShapeDtypeStruct((node_dev, width), bf16),
-        in_specs=[smem] + [vmem] * 4 + [pl.BlockSpec(memory_space=pltpu.HBM)],
+        out_shape=pltpu.VMEM((node_dev, width), bf16),
+        in_specs=[smem] + [vmem] * 2 + [pl.BlockSpec(memory_space=pltpu.HBM)] * 3,
         out_specs=vmem,
         scratch_shapes=[pltpu.VMEM((n_row * node_dev // tile, tile, LANES), bf16)] * phases
         + [pltpu.VMEM((2 * n_q * half, LANES), bf16)] * phases
         + [pltpu.VMEM((2 * (n_q - 1) * half, LANES), bf16)] * phases
         + [
+            pltpu.VMEM((node_dev, width), bf16),
+            pltpu.VMEM((width, width), bf16),
             pltpu.VMEM((slots + 1, tile, tile), bf16),
             pltpu.VMEM((pairs_total + 1, tile, LANES), bf16),
             pltpu.VMEM((n_col * node_dev, LANES), bf16),
@@ -406,9 +444,10 @@
             pltpu.SMEM((8, plan_width), jnp.int32),
             pltpu.SMEM((8, plan_width), jnp.float32),
             dma((2,)),
+            dma((1 + PARTS,)),
             dma((LOADS,)),
-            dma((phases, 2, n_row - 1, PARTS)),
-            dma((phases, 2, n_row - 1, PARTS)),
+            dma((phases, 2 * n_row - 1, PARTS)),
+            dma((phases, 2 * n_row - 1, PARTS)),
             dma((phases, 2, 2)),
             dma((phases, 2, 2)),
             dma((phases, 2, steps, 2)),

time: 101 us -> 96.1 us (0.951)
  Pallas kernels: 98.1 us -> 94.1 us
  matrix products: 2.13 us -> 1.09 us
    pallas_call x1, Pallas kernels: 98.1 us -> 94.1 us  [shards(): pl.pallas_call(functools.partial(kernel, n_row, n_col, chunks, pairs_tota...]
    dot_general x1, matrix products: 2.13 us -> 1.09 us  [shards(): product = jnp.dot(aggregate, w_second, preferred_element_type=jnp.float32)]
where the time goes in v2:
time: 96.1 us; the launch traced here: 95.9 us
  Pallas kernels  94.1 us (98%)
  matrix products  1.09 us (1%)
    pallas_call x1, Pallas kernels, shards(): pl.pallas_call(functools.partial(kernel, n_row, n_col, chunks, pairs_tota...  94.1 us

profile of v2, /device:TPU:0, one launch (start us, length us, event | category | flops | bytes accessed | tf_op | source)
XLA Modules:
  0.0 95.9 jit_solution(4124431943575551282)
XLA Ops:
  0.0 0.0 copy-start
  0.7 94.1 %gcn.1 = bf16[1024,256]{1,0:T(8,128)(2,1)S(1)} custom-call(s32[1,1]{1,0:T(1,128)S(6)} %copy.8.filled, s32[1,256]{1,0:T(1,128)} %bitcast.6, s32[1,256]{1,0:T(1,128)} %bitcast.7, bf16[1024,256]{1,0:T(8,128)(2,1)} %feat_hbm.1, bf16[256,256]{1,0:T(8,128)(2,1)} %w1_hbm.1, bf16[256,128,128]{2,1,0:T(8,128)(2,1)} %bitcast.5), custom_call_target="tpu_custom_call" | custom-call | tf_op jit(solution)/shard_map/gcn/pallas_call | solution.py:427
  94.8 0.0 copy-done
  94.8 1.1 %fusion = bf16[1024,256]{1,0:T(8,128)(2,1)} fusion(bf16[1024,256]{1,0:T(8,128)(2,1)S(1)} %gcn.1, bf16[256,256]{1,0:T(8,128)(2,1)S(1)} %copy-done), kind=kOutput, calls=%fused_computation.1 | convolution fusion | flops 134742016 | bytes 1179648 | tf_op jit(solution)/shard_map/dot_general | solution.py:460
Async XLA Ops:
  0.0 94.8 %copy-start = (bf16[256,256]{1,0:T(8,128)(2,1)S(1)}, bf16[256,256]{1,0:T(8,128)(2,1)}, u32[]{:S(2)}) copy-start(bf16[256,256]{1,0:T(8,128)(2,1)} %param.13) | copy-start | bytes 393220

commit v3 on v2

--- a/solution.py
+++ b/solution.py
@@ -10,6 +10,7 @@
 LANES = 128
 UNROLL_PARTS = 2
 LOADS = 4
+SETS = 3
 PARTS = 2
 ROWS_AT_ONCE = 256
 MESH = pl.DeviceIdType.MESH
@@ -54,20 +55,21 @@
 
 
 def kernel(n_row, n_col, chunks, pairs_total, filled, row_ids, col_ids, feat_hbm, w1_hbm, vals_hbm, out, *scratch):
-    phases = 2 * chunks
+    phases = 2 * chunks + 1
+    first, second = phases - 2, phases - 1
     panels = scratch[:phases]
     core_in = scratch[phases : 2 * phases]
     step_in = scratch[2 * phases : 3 * phases]
-    feat, w1, vals, sums, part, plan_v, keep_v, plan, keep, plan_sem = scratch[3 * phases : 3 * phases + 10]
-    in_sem, load_sem, g_send, g_recv, c_send, c_recv, s_send, s_recv = scratch[3 * phases + 10 :]
+    feat, w1, vals, sums, wide_part, thin_part, spread, held = scratch[3 * phases : 3 * phases + 8]
+    plan_v, keep_v, plan, keep, plan_sem = scratch[3 * phases + 8 : 3 * phases + 13]
+    in_sem, load_sem, g_send, g_recv, c_send, c_recv, s_send, s_recv = scratch[3 * phases + 13 :]
     slots, tile, _ = vals_hbm.shape
     node_dev, width = feat.shape
     per_dev = node_dev // tile
     half_tiles = per_dev // 2
     n_q = n_col // 2
     steps = n_q.bit_length() - 1
-    block = half_tiles * tile
-    half_rows = n_q * block
+    low = iota((tile, LANES), 1) < LANES // 2
     r, c = lax.axis_index("row"), lax.axis_index("col")
     b0 = lax.rem(c, 2)
     q = lax.div(c, 2)
@@ -122,8 +124,14 @@
     for load in loads:
         load.start()
 
+    def node_tiles(phase):
+        return per_dev // 2 if phase >= first else per_dev
+
     def own(phase, offset, rows):
-        return panels[phase].at[pl.ds(r * per_dev + offset, rows)]
+        return panels[phase].at[pl.ds(r * node_tiles(phase) + offset, rows)]
+
+    def turned(value):
+        return pltpu.roll(value, LANES // 2, 1)
 
     def project(chunk, k):
         size = min(cut_rows, ROWS_AT_ONCE)
@@ -136,19 +144,25 @@
             tiles = size // tile
             own(chunk, at // tile, tiles)[...] = product.astype(jnp.bfloat16).reshape(tiles, tile, LANES)
 
+    def way(d):
+        return d - 1 if d > 0 else last_row - 1 - d
+
     def node_copy(phase, origin, d, k, device):
-        view = panels[phase].at[pl.ds(origin * per_dev + k * cut, cut)]
+        share = node_tiles(phase) // PARTS
+        view = panels[phase].at[pl.ds(origin * node_tiles(phase) + k * share, share)]
         return pltpu.make_async_remote_copy(
             src_ref=view,
             dst_ref=view,
-            send_sem=g_send.at[phase, d + n_row - 1, k],
-            recv_sem=g_recv.at[phase, d + n_row - 1, k],
+            send_sem=g_send.at[phase % SETS, way(d), k],
+            recv_sem=g_recv.at[phase, way(d), k],
             device_id=(device, c),
             device_id_type=MESH,
         )
 
-    def inner_sends(phase, k):
+    def inner_sends(phase, k, reaches=range(1, n_row)):
         for d in distances:
+            if abs(d) not in reaches:
+                continue
             target = r + d
             yield inner(target), node_copy(phase, r, d, k, target)
 
@@ -171,9 +185,9 @@
             pl.when(valid)(copy.start)
 
     def own_inner(phase):
-        if phase < phases:
+        for reach in range(last_row, 0, -1):
             for k in range(PARTS):
-                start_all(inner_sends(phase, k))
+                start_all(inner_sends(phase, k, (reach,)))
 
     def own_outer(phase):
         if phase < phases:
@@ -190,22 +204,49 @@
                     forward.start()
 
     def relay_far(phase):
+        for near in range(2, last_row):
+            for k in range(PARTS):
+                relay(phase, near, k)
+
+    def relay_near(phase):
         for k in range(PARTS):
-            for near in range(2, last_row):
-                relay(phase, near, k)
+            relay(phase, 1, k)
 
     def relay_all(phase):
-        for k in range(PARTS):
-            for near in range(1, last_row):
-                relay(phase, near, k)
+        relay_near(phase)
+        relay_far(phase)
+
+    def arrive(phase, d, k):
+        origin = r - d
+        relayed = r == (n_row - 2 if d > 0 else 1)
+        valid = (origin >= 0) & (origin <= last_row) & jnp.logical_not(relayed)
+        pl.when(valid)(node_copy(phase, origin, d, k, r).wait_recv)
 
     def gathered(phase):
         for k in range(PARTS):
             for d in sorted(distances, key=abs):
-                origin = r - d
-                relayed = r == (n_row - 2 if d > 0 else 1)
-                valid = (origin >= 0) & (origin <= last_row) & jnp.logical_not(relayed)
-                pl.when(valid)(node_copy(phase, origin, d, k, r).wait_recv)
+                arrive(phase, d, k)
+
+    def spread_node(phase, origin):
+        def body(i, carry):
+            at = origin * (per_dev // 2) + i
+            pair = panels[phase][at].astype(jnp.float32)
+            other = turned(pair)
+            spread[2 * at] = jnp.where(low, pair, other).astype(jnp.bfloat16)
+            spread[2 * at + 1] = jnp.where(low, other, pair).astype(jnp.bfloat16)
+            return carry
+
+        lax.fori_loop(0, per_dev // 2, body, 0, unroll=True)
+
+    def gathered_spread(phase):
+        spread_node(phase, r)
+        for d in sorted(distances, key=abs):
+            for k in range(PARTS):
+                arrive(phase, d, k)
+
+            @pl.when((r - d >= 0) & (r - d <= last_row))
+            def _(d=d):
+                spread_node(phase, r - d)
 
     def drain(phase):
         for k in range(PARTS):
@@ -217,9 +258,7 @@
 
     unroll = pairs_total // UNROLL_PARTS
 
-    def compute(phase):
-        panel = panels[phase]
-
+    def compute(panel, low_trip=0, high_trip=UNROLL_PARTS, total=None):
         def one(p, acc):
             left = [vals[plan[0, 2 * p + k]] for k in range(2)]
             right = [panel[plan[1, 2 * p + k]] for k in range(2)]
@@ -237,23 +276,31 @@
                 acc = one(i * unroll + u, acc)
             return acc
 
-        lax.fori_loop(0, UNROLL_PARTS, body, jnp.zeros((tile, LANES), jnp.float32))
-
-    def place_rows(parity, h, at, count):
+        if total is None:
+            total = jnp.zeros((tile, LANES), jnp.float32)
+        return lax.fori_loop(low_trip, high_trip, body, total)
+
+    def place_rows(part, region, parity, h, at, count, narrow):
+        taken = half_tiles // 2 if narrow else half_tiles
+
         def body(i, carry):
             rev = sum(lax.rem(lax.div(at + i, 1 << k), 2) * (1 << (steps - 1 - k)) for k in range(steps))
             dest = 2 * (rev if h == 0 else at + i) + parity
-            base = ((parity * 2 + h) * n_q + at + i) * half_tiles
-            for t in range(half_tiles):
-                row_tile = dest * per_dev + h * half_tiles + t
-                part[pl.ds(pl.multiple_of((base + t) * tile, tile), tile), :] = sums[
-                    plan[2, row_tile]
-                ]
+            base = region + ((parity * 2 + h) * n_q + at + i) * taken
+            row_tile = dest * per_dev + h * half_tiles
+            for t in range(taken):
+                if narrow:
+                    rows = jnp.where(
+                        low, sums[plan[2, row_tile + 2 * t]], sums[plan[2, row_tile + 2 * t + 1]]
+                    )
+                else:
+                    rows = sums[plan[2, row_tile + t]]
+                part[pl.ds(pl.multiple_of((base + t) * tile, tile), tile), :] = rows
             return carry
 
         lax.fori_loop(0, count, body, 0)
 
-    def add_in(at, source, source_at, rows):
+    def add_in(part, at, source, source_at, rows):
         piece = min(rows, ROWS_AT_ONCE)
 
         def body(i, carry):
@@ -287,19 +334,63 @@
         mine = mine_at(h, step)
         return [((1 - mine) * (size // 2), size // 2), (mine * (size // 2), size // 2)]
 
-    def reduce(phase):
-        started = []
+    def tile_sum(part, at, source, source_at, t):
+        here = pl.ds(pl.multiple_of(at + t * tile, tile), tile)
+        there = pl.ds(pl.multiple_of(source_at + t * tile, tile), tile)
+        return part[here, :].astype(jnp.float32) + source[there, :].astype(jnp.float32)
+
+    def finish(part, phase, h, at, source, source_at):
+        if phase == chunks - 1:
+            for t in range(half_tiles // 2):
+                even, odd = (
+                    jnp.maximum(tile_sum(part, at, source, source_at, 2 * t + i), 0.0) for i in range(2)
+                )
+                for made, value in (
+                    (first, jnp.where(low, even, turned(odd))),
+                    (second, jnp.where(low, turned(even), odd)),
+                ):
+                    own(made, h * (half_tiles // 2) + t, 1)[...] = value.astype(jnp.bfloat16)[None]
+        elif phase < chunks:
+            for t in range(half_tiles):
+                hidden = jnp.maximum(tile_sum(part, at, source, source_at, t), 0.0).astype(jnp.bfloat16)
+                own(phase + chunks, h * half_tiles + t, 1)[...] = hidden[None]
+        elif phase < first:
+            lanes = (phase - chunks) * LANES
+            for t in range(half_tiles):
+                rows = (h * half_tiles + t) * tile
+                added = tile_sum(part, at, source, source_at, t)
+                out[rows : rows + tile, lanes : lanes + LANES] = added.astype(jnp.bfloat16)
+        else:
+            lanes = (chunks - 1) * LANES
+            for t in range(half_tiles // 2):
+                rows = (h * (half_tiles // 2) + t) * tile
+                added = tile_sum(part, at, source, source_at, t)
+                if phase == first:
+                    held[rows : rows + tile, :] = added.astype(jnp.bfloat16)
+                else:
+                    before = held[rows : rows + tile, :].astype(jnp.float32)
+                    even = jnp.where(low, before, turned(added)).astype(jnp.bfloat16)
+                    odd = jnp.where(low, turned(before), added).astype(jnp.bfloat16)
+                    out[2 * rows : 2 * rows + tile, lanes : lanes + LANES] = even
+                    out[2 * rows + tile : 2 * (rows + tile), lanes : lanes + LANES] = odd
+
+    def reduce(phase, started):
+        narrow = phase >= first
+        part = thin_part if narrow else wide_part
+        block = node_tiles(phase) // 2 * tile
+        half_rows = n_q * block
+        region = 4 * half_rows if phase == second else 0
         cuts = [pieces(h, 0, half_rows) for h in range(2)]
         arrived = [[], []]
         for k in range(len(cuts[0])):
             for h in range(2):
                 off, rows = cuts[h][k]
-                place_rows(1 - b0, h, lax.div(off, block), rows // block)
+                place_rows(part, region // tile, 1 - b0, h, lax.div(off, block), rows // block, narrow)
                 copy = remote(
-                    rows_at(part, ((1 - b0) * 2 + h) * half_rows + off, rows),
+                    rows_at(part, region + ((1 - b0) * 2 + h) * half_rows + off, rows),
                     rows_at(core_in[phase], h * half_rows + off, rows),
-                    c_send.at[phase, h, k],
-                    c_recv.at[phase, h, k],
+                    c_send.at[phase % SETS, h, k],
+                    c_recv.at[phase % SETS, h, k],
                     partners[0],
                 )
                 copy.start()
@@ -308,13 +399,14 @@
         for k in range(len(cuts[0])):
             for h in range(2):
                 off, rows = cuts[h][k]
-                place_rows(b0, h, lax.div(off, block), rows // block)
-        base = [(b0 * 2 + h) * half_rows for h in range(2)]
+                place_rows(part, region // tile, b0, h, lax.div(off, block), rows // block, narrow)
+        base = [region + (b0 * 2 + h) * half_rows for h in range(2)]
+        yield
 
         def take(h, k):
             copy, source, source_at, off, rows = arrived[h][k]
             copy.wait_recv()
-            add_in(base[h] + off, source, source_at, rows)
+            add_in(part, base[h] + off, source, source_at, rows)
 
         size = half_rows
         for step in range(steps):
@@ -328,36 +420,30 @@
                     copy = remote(
                         rows_at(part, away + off, rows),
                         rows_at(step_in[phase], landing + off, rows),
-                        s_send.at[phase, h, step, k],
-                        s_recv.at[phase, h, step, k],
+                        s_send.at[phase % SETS, h, step, k],
+                        s_recv.at[phase % SETS, h, step, k],
                         partners[1 + bit],
                     )
                     copy.start()
                     started.append(copy)
                     following[h].append((copy, step_in[phase], landing + off, off, rows))
+            if step == steps - 1:
+                yield
             for h in range(2):
                 take(h, 1)
                 base[h] = base[h] + mine_at(h, step) * (size // 2)
             size //= 2
             arrived = following
+            if step == 0 and phase < first - 1:
+                relay_near(phase + 1)
+                if phase + 1 < chunks:
+                    relay_far(phase + 1)
             if step == 0:
-                for k in range(PARTS):
-                    relay(phase + 1, 1, k)
+                yield
         for h in range(2):
             copy, source, source_at, off, rows = arrived[h][0]
             copy.wait_recv()
-            here = pl.ds(pl.multiple_of(base[h], tile), block)
-            there = pl.ds(pl.multiple_of(source_at, tile), block)
-            added = part[here, :].astype(jnp.float32) + source[there, :].astype(jnp.float32)
-            if phase < chunks:
-                hidden = jnp.maximum(added, 0.0).astype(jnp.bfloat16)
-                own(phase + chunks, h * half_tiles, half_tiles)[...] = hidden.reshape(
-                    half_tiles, tile, LANES
-                )
-            else:
-                at = (phase - chunks) * LANES
-                out[h * block : (h + 1) * block, at : at + LANES] = added.astype(jnp.bfloat16)
-        return started
+            finish(part, phase, h, base[h], source, source_at)
 
     w1_load.wait()
     for k in range(PARTS):
@@ -365,8 +451,10 @@
         project(0, k)
         if k == 0:
             pl.semaphore_wait(barrier, greeted)
-        start_all(inner_sends(0, k))
+        start_all(inner_sends(0, k, (1,)))
         start_all(outer_sends(0, k))
+    for k in range(PARTS):
+        start_all(inner_sends(0, k, range(2, n_row)))
     for chunk in range(1, chunks):
         for k in range(PARTS):
             project(chunk, k)
@@ -393,19 +481,58 @@
         load.wait()
     pl.when(inner(r))(lambda: own_inner(1))
     own_outer(1)
-    for phase in range(phases):
+    started = []
+    for phase in range(first):
         gathered(phase)
-        compute(phase)
-        started = reduce(phase)
+        if phase == first - 1:
+            relay_near(first)
+            own_outer(second)
+        compute(panels[phase])
+        work = reduce(phase, started)
+        if phase == first - 1:
+            break
+        for _ in work:
+            pass
+        made = []
         if phase < chunks:
-            own_inner(phase + chunks)
-        if phase + 1 < phases:
+            made = [first, second] if phase == chunks - 1 else [phase + chunks]
+        for later in made:
+            if later >= SETS:
+                drain(later - SETS)
+            own_inner(later)
+        if phase + 1 >= chunks:
             relay_far(phase + 1)
-        if phase < chunks:
-            own_outer(phase + chunks)
+        for later in made[:1]:
+            own_outer(later)
         for copy in started:
             copy.wait_send()
-    for phase in range(phases):
+        started.clear()
+    next(work)
+    next(work)
+    relay_far(first)
+    relay_near(second)
+    next(work)
+    gathered_spread(first)
+    compute(spread)
+    relay_far(second)
+    work_first = reduce(first, started)
+    next(work_first)
+    next(work_first)
+    for _ in work:
+        pass
+    gathered_spread(second)
+    total = compute(spread, 0, UNROLL_PARTS // 2)
+    next(work_first)
+    compute(spread, UNROLL_PARTS // 2, UNROLL_PARTS, total)
+    work_second = reduce(second, started)
+    next(work_second)
+    next(work_second)
+    for rest in (work_first, work_second):
+        for _ in rest:
+            pass
+    for copy in started:
+        copy.wait_send()
+    for phase in range(phases - SETS, phases):
         drain(phase)
 
 
@@ -414,7 +541,8 @@
     node_dev, width = features.shape
     row_tiles = node_dev * n_col // tile
     chunks = width // LANES
-    phases = 2 * chunks
+    phases = 2 * chunks + 1
+    shares = [1] * (phases - 2) + [2, 2]
     pairs_total = -(-(slots + row_tiles) // (2 * UNROLL_PARTS)) * UNROLL_PARTS
     n_q = n_col // 2
     steps = n_q.bit_length() - 1
@@ -430,15 +558,18 @@
         out_shape=pltpu.VMEM((node_dev, width), bf16),
         in_specs=[smem] + [vmem] * 2 + [pl.BlockSpec(memory_space=pltpu.HBM)] * 3,
         out_specs=vmem,
-        scratch_shapes=[pltpu.VMEM((n_row * node_dev // tile, tile, LANES), bf16)] * phases
-        + [pltpu.VMEM((2 * n_q * half, LANES), bf16)] * phases
-        + [pltpu.VMEM((2 * (n_q - 1) * half, LANES), bf16)] * phases
+        scratch_shapes=[pltpu.VMEM((n_row * node_dev // tile // share, tile, LANES), bf16) for share in shares]
+        + [pltpu.VMEM((2 * n_q * half // share, LANES), bf16) for share in shares]
+        + [pltpu.VMEM((2 * (n_q - 1) * half // share, LANES), bf16) for share in shares]
         + [
             pltpu.VMEM((node_dev, width), bf16),
             pltpu.VMEM((width, width), bf16),
             pltpu.VMEM((slots + 1, tile, tile), bf16),
             pltpu.VMEM((pairs_total + 1, tile, LANES), bf16),
             pltpu.VMEM((n_col * node_dev, LANES), bf16),
+            pltpu.VMEM((n_col * node_dev, LANES), bf16),
+            pltpu.VMEM((n_row * node_dev // tile, tile, LANES), bf16),
+            pltpu.VMEM((node_dev // 2, LANES), bf16),
             pltpu.VMEM((8, plan_width), jnp.int32),
             pltpu.VMEM((8, plan_width), jnp.float32),
             pltpu.SMEM((8, plan_width), jnp.int32),
@@ -446,12 +577,12 @@
             dma((2,)),
             dma((1 + PARTS,)),
             dma((LOADS,)),
-            dma((phases, 2 * n_row - 1, PARTS)),
-            dma((phases, 2 * n_row - 1, PARTS)),
-            dma((phases, 2, 2)),
-            dma((phases, 2, 2)),
-            dma((phases, 2, steps, 2)),
-            dma((phases, 2, steps, 2)),
+            dma((SETS, 2 * n_row - 2, PARTS)),
+            dma((phases, 2 * n_row - 2, PARTS)),
+            dma((SETS, 2, 2)),
+            dma((SETS, 2, 2)),
+            dma((SETS, 2, steps, 2)),
+            dma((SETS, 2, steps, 2)),
         ],
         compiler_params=pltpu.CompilerParams(
             collective_id=0, has_side_effects=True, vmem_limit_bytes=63 * 1024 * 1024

time: 96.1 us -> 91.6 us (0.953)
  Pallas kernels: 94.1 us -> 89.7 us
    pallas_call x1, Pallas kernels: 94.1 us -> 89.7 us  [shards(): pl.pallas_call(functools.partial(kernel, n_row, n_col, chunks, pairs_tota...]
where the time goes in v3:
time: 91.6 us; the launch traced here: 91.5 us
  Pallas kernels  89.7 us (98%)
  matrix products  1.09 us (1%)
    pallas_call x1, Pallas kernels, shards(): pl.pallas_call(functools.partial(kernel, n_row, n_col, chunks, pairs_tota...  89.7 us

profile of v3, /device:TPU:0, one launch (start us, length us, event | category | flops | bytes accessed | tf_op | source)
XLA Modules:
  0.0 91.5 jit_solution(10148095433541547733)
XLA Ops:
  0.0 0.0 copy-start
  0.7 89.7 %gcn.1 = bf16[1024,256]{1,0:T(8,128)(2,1)S(1)} custom-call(s32[1,1]{1,0:T(1,128)S(6)} %copy.8.filled, s32[1,256]{1,0:T(1,128)} %bitcast.6, s32[1,256]{1,0:T(1,128)} %bitcast.7, bf16[1024,256]{1,0:T(8,128)(2,1)} %feat_hbm.1, bf16[256,256]{1,0:T(8,128)(2,1)} %w1_hbm.1, bf16[256,128,128]{2,1,0:T(8,128)(2,1)} %bitcast.5), custom_call_target="tpu_custom_call" | custom-call | tf_op jit(solution)/shard_map/gcn/pallas_call | solution.py:555
  90.4 0.0 copy-done
  90.4 1.1 %fusion = bf16[1024,256]{1,0:T(8,128)(2,1)} fusion(bf16[1024,256]{1,0:T(8,128)(2,1)S(1)} %gcn.1, bf16[256,256]{1,0:T(8,128)(2,1)S(1)} %copy-done), kind=kOutput, calls=%fused_computation.1 | convolution fusion | flops 134742016 | bytes 1179648 | tf_op jit(solution)/shard_map/dot_general | solution.py:591
Async XLA Ops:
  0.0 90.4 %copy-start = (bf16[256,256]{1,0:T(8,128)(2,1)S(1)}, bf16[256,256]{1,0:T(8,128)(2,1)}, u32[]{:S(2)}) copy-start(bf16[256,256]{1,0:T(8,128)(2,1)} %param.13) | copy-start | bytes 393220

commit v4 on v3

--- a/solution.py
+++ b/solution.py
@@ -54,15 +54,15 @@
     return slot_at, col_at, keep.astype(jnp.float32), last
 
 
-def kernel(n_row, n_col, chunks, pairs_total, filled, row_ids, col_ids, feat_hbm, w1_hbm, vals_hbm, out, *scratch):
+def kernel(n_row, n_col, chunks, pairs_total, filled_hbm, rows_hbm, cols_hbm, feat_hbm, w1_hbm, vals_hbm, out, *scratch):
     phases = 2 * chunks + 1
     first, second = phases - 2, phases - 1
     panels = scratch[:phases]
     core_in = scratch[phases : 2 * phases]
     step_in = scratch[2 * phases : 3 * phases]
     feat, w1, vals, sums, wide_part, thin_part, spread, held = scratch[3 * phases : 3 * phases + 8]
-    plan_v, keep_v, plan, keep, plan_sem = scratch[3 * phases + 8 : 3 * phases + 13]
-    in_sem, load_sem, g_send, g_recv, c_send, c_recv, s_send, s_recv = scratch[3 * phases + 13 :]
+    filled, row_ids, col_ids, plan_v, keep_v, plan, keep, plan_sem = scratch[3 * phases + 8 : 3 * phases + 16]
+    in_sem, load_sem, g_send, g_recv, c_send, c_recv, s_send, s_recv = scratch[3 * phases + 16 :]
     slots, tile, _ = vals_hbm.shape
     node_dev, width = feat.shape
     per_dev = node_dev // tile
@@ -86,6 +86,14 @@
     w1_load.start()
     for load in feat_loads:
         load.start()
+    id_loads = [
+        pltpu.make_async_copy(source, target, in_sem.at[1 + PARTS + i])
+        for i, (source, target) in enumerate(
+            [(filled_hbm, filled), (rows_hbm, row_ids), (cols_hbm, col_ids)]
+        )
+    ]
+    for load in id_loads:
+        load.start()
 
     barrier = pltpu.get_barrier_semaphore()
     partners = []
@@ -154,7 +162,7 @@
             src_ref=view,
             dst_ref=view,
             send_sem=g_send.at[phase % SETS, way(d), k],
-            recv_sem=g_recv.at[phase, way(d), k],
+            recv_sem=g_recv.at[phase, origin if d > 0 else origin - 1, k],
             device_id=(device, c),
             device_id_type=MESH,
         )
@@ -461,8 +469,10 @@
     pl.when(outer(r))(lambda: own_inner(1))
     vals[slots] = jnp.zeros((tile, tile), vals.dtype)
     sums[pairs_total] = jnp.zeros((tile, LANES), sums.dtype)
+    for load in id_loads:
+        load.wait()
     slot_at, col_at, keep_at, last = pair_plan(
-        row_ids[...], col_ids[...], filled[0, 0], n_col * per_dev, pairs_total, plan.shape[1]
+        row_ids[...], col_ids[...], filled[...], n_col * per_dev, pairs_total, plan.shape[1]
     )
     plan_v[0:1, :] = slot_at
     plan_v[1:2, :] = col_at
@@ -486,7 +496,6 @@
         gathered(phase)
         if phase == first - 1:
             relay_near(first)
-            own_outer(second)
         compute(panels[phase])
         work = reduce(phase, started)
         if phase == first - 1:
@@ -510,6 +519,7 @@
     next(work)
     next(work)
     relay_far(first)
+    own_outer(second)
     relay_near(second)
     next(work)
     gathered_spread(first)
@@ -549,14 +559,13 @@
     plan_width = -(-2 * pairs_total // LANES) * LANES
     half = node_dev // 2
     vmem = pl.BlockSpec(memory_space=pltpu.VMEM)
-    smem = pl.BlockSpec(memory_space=pltpu.SMEM)
     bf16 = jnp.bfloat16
     dma = pltpu.SemaphoreType.DMA
     aggregate = pl.pallas_call(
         functools.partial(kernel, n_row, n_col, chunks, pairs_total),
         name="gcn",
         out_shape=pltpu.VMEM((node_dev, width), bf16),
-        in_specs=[smem] + [vmem] * 2 + [pl.BlockSpec(memory_space=pltpu.HBM)] * 3,
+        in_specs=[pl.BlockSpec(memory_space=pltpu.HBM)] * 6,
         out_specs=vmem,
         scratch_shapes=[pltpu.VMEM((n_row * node_dev // tile // share, tile, LANES), bf16) for share in shares]
         + [pltpu.VMEM((2 * n_q * half // share, LANES), bf16) for share in shares]
@@ -570,15 +579,18 @@
             pltpu.VMEM((n_col * node_dev, LANES), bf16),
             pltpu.VMEM((n_row * node_dev // tile, tile, LANES), bf16),
             pltpu.VMEM((node_dev // 2, LANES), bf16),
+            pltpu.VMEM((1, 1), jnp.int32),
+            pltpu.VMEM((1, slots), jnp.int32),
+            pltpu.VMEM((1, slots), jnp.int32),
             pltpu.VMEM((8, plan_width), jnp.int32),
             pltpu.VMEM((8, plan_width), jnp.float32),
             pltpu.SMEM((8, plan_width), jnp.int32),
             pltpu.SMEM((8, plan_width), jnp.float32),
             dma((2,)),
-            dma((1 + PARTS,)),
+            dma((4 + PARTS,)),
             dma((LOADS,)),
             dma((SETS, 2 * n_row - 2, PARTS)),
-            dma((phases, 2 * n_row - 2, PARTS)),
+            dma((phases, n_row - 1, PARTS)),
             dma((SETS, 2, 2)),
             dma((SETS, 2, 2)),
             dma((SETS, 2, steps, 2)),

time: 91.6 us -> 90.2 us (0.985)
  Pallas kernels: 89.7 us -> 88.2 us
    pallas_call x1, Pallas kernels: 89.7 us -> 88.2 us  [shards(): pl.pallas_call(functools.partial(kernel, n_row, n_col, chunks, pairs_tota...]
where the time goes in v4:
time: 90.2 us; the launch traced here: 90 us
  Pallas kernels  88.2 us (98%)
  matrix products  1.09 us (1%)
    pallas_call x1, Pallas kernels, shards(): pl.pallas_call(functools.partial(kernel, n_row, n_col, chunks, pairs_tota...  88.2 us

profile of v4, /device:TPU:0, one launch (start us, length us, event | category | flops | bytes accessed | tf_op | source)
XLA Modules:
  0.0 90.0 jit_solution(4695193091454203735)
XLA Ops:
  0.0 0.0 copy-start
  0.7 88.2 %gcn.1 = bf16[1024,256]{1,0:T(8,128)(2,1)S(1)} custom-call(s32[1,1]{1,0:T(1,128)S(6)} %copy.8.filled_hbm, s32[1,256]{1,0:T(1,128)} %bitcast.6, s32[1,256]{1,0:T(1,128)} %bitcast.7, bf16[1024,256]{1,0:T(8,128)(2,1)} %feat_hbm.1, bf16[256,256]{1,0:T(8,128)(2,1)} %w1_hbm.1, bf16[256,128,128]{2,1,0:T(8,128)(2,1)} %bitcast.5), custom_call_target="tpu_custom_call" | custom-call | tf_op jit(solution)/shard_map/gcn/pallas_call | solution.py:564
  88.9 0.0 copy-done
  88.9 1.1 %fusion = bf16[1024,256]{1,0:T(8,128)(2,1)} fusion(bf16[1024,256]{1,0:T(8,128)(2,1)S(1)} %gcn.1, bf16[256,256]{1,0:T(8,128)(2,1)S(1)} %copy-done), kind=kOutput, calls=%fused_computation.1 | convolution fusion | flops 134742016 | bytes 1179648 | tf_op jit(solution)/shard_map/dot_general | solution.py:603
Async XLA Ops:
  0.0 88.9 %copy-start = (bf16[256,256]{1,0:T(8,128)(2,1)S(1)}, bf16[256,256]{1,0:T(8,128)(2,1)}, u32[]{:S(2)}) copy-start(bf16[256,256]{1,0:T(8,128)(2,1)} %param.13) | copy-start | bytes 393220
